TPU v7x, 32 devices: a whole 2x2x4 slice. The times are simulated.
32 devices in a mesh: dp: 16 (over z, y, core), seq: 2 (over x).
Axes of the slice: x: 2, y: 2, z: 4, core: 2. Of those that a mesh axis runs over, the one named last changes fastest.
Arguments:
- tokens: bfloat16 [17664, 1024], P(('dp', 'seq')), may hold values from -6 to 6
- skipped: bfloat16 [17664, 1024], P(('dp', 'seq')), may hold values from -6 to 6
- cotangent: bfloat16 [17664, 1024], P(('dp', 'seq')), may hold values from -6 to 6
- merge_weight: bfloat16 [2048, 1024], P('dp'), may hold values from -0.125 to 0.125
- merge_bias: bfloat16 [1024], P('dp'), may hold values from -2 to 2
- first_gain: bfloat16 [1024], P('dp'), may hold values from 0.099609375 to 1.8984375
- first_shift: bfloat16 [1024], P('dp'), may hold values from -2 to 2
- project_in: bfloat16 [1024, 3072], P('dp'), may hold values from -0.1875 to 0.1875
- project_out: bfloat16 [1024, 1024], P('dp'), may hold values from -1.5 to 1.5
- project_bias: bfloat16 [1024], P('dp'), may hold values from -2 to 2
- second_gain: bfloat16 [1024], P('dp'), may hold values from 0.099609375 to 1.8984375
- second_shift: bfloat16 [1024], P('dp'), may hold values from -2 to 2
- expand_weight: bfloat16 [1024, 4096], P('dp'), may hold values from -0.1875 to 0.1875
- expand_bias: bfloat16 [4096], P('dp'), may hold values from -2 to 2
- reduce_weight: bfloat16 [4096, 1024], P('dp'), may hold values from -0.09375 to 0.09375
- reduce_bias: bfloat16 [1024], P('dp'), may hold values from -2 to 2
Outputs:
- output: bfloat16 [17664, 1024], P(('dp', 'seq'))
- tokens_grad: float32 [17664, 1024], P(('dp', 'seq'))
- skipped_grad: float32 [17664, 1024], P(('dp', 'seq'))
- merge_weight_grad: float32 [2048, 1024], P('dp')
- project_in_grad: float32 [1024, 3072], P('dp')
- project_out_grad: float32 [1024, 1024], P('dp')
- expand_weight_grad: float32 [1024, 4096], P('dp')
- reduce_weight_grad: float32 [4096, 1024], P('dp')
- merge_bias_grad: float32 [1024], P('dp')
- first_gain_grad: float32 [1024], P('dp')
- first_shift_grad: float32 [1024], P('dp')
- project_bias_grad: float32 [1024], P('dp')
- second_gain_grad: float32 [1024], P('dp')
- second_shift_grad: float32 [1024], P('dp')
- expand_bias_grad: float32 [4096], P('dp')
- reduce_bias_grad: float32 [1024], P('dp')
All inputs are finite; a program needn't handle non-finite values.
Results may differ from a plain program's by a relative error of at most 0.012.
Values may be sent and summed in bfloat16 or wider, within the bound.
A program may use at most 320 MiB of HBM per device.

v0:
```python
from functools import partial

import jax
import jax.numpy as jnp
from jax import lax
from jax.sharding import PartitionSpec as P

HD = 64
LEN = 1104


EPSILON = 1e-05
BF = jnp.bfloat16
FL = jnp.float32


def norm_apply(stream, gain, shift):
    centred = stream - jnp.mean(stream, -1, keepdims=True)
    variance = jnp.mean(centred * centred, -1, keepdims=True)
    return centred * lax.rsqrt(variance + EPSILON) * gain + shift


def attend_forward(block):
    queries, key_rows, values = block
    scale = HD ** (-0.5)
    scores = jnp.einsum("qhd,khd->hqk", queries, key_rows, preferred_element_type=FL) * scale
    highest = jnp.max(scores, -1, keepdims=True)
    expo = jnp.exp(scores - highest)
    total = jnp.sum(expo, -1, keepdims=True)
    probs_low = (expo / total).astype(BF)
    mixed = jnp.einsum("hqk,khd->qhd", probs_low, values, preferred_element_type=FL)
    return (mixed.astype(BF), (highest + jnp.log(total))[..., 0])


def attend_backward(block):
    queries, key_rows, values, grad_mixed, logsum = block
    scale = HD ** (-0.5)
    scores = jnp.einsum("qhd,khd->hqk", queries, key_rows, preferred_element_type=FL) * scale
    probs = jnp.exp(scores - logsum[..., None])
    probs_low = probs.astype(BF)
    grad_values = jnp.einsum("hqk,qhd->khd", probs_low, grad_mixed, preferred_element_type=FL)
    grad_probs = jnp.einsum("qhd,khd->hqk", grad_mixed, values, preferred_element_type=FL)
    row_dot = jnp.sum(grad_probs * probs, -1, keepdims=True)
    grad_scores = (probs * (grad_probs - row_dot)).astype(BF)
    grad_queries = (
        jnp.einsum("hqk,khd->qhd", grad_scores, key_rows, preferred_element_type=FL) * scale
    )
    grad_keys = jnp.einsum("hqk,qhd->khd", grad_scores, queries, preferred_element_type=FL) * scale
    return jnp.stack([grad_queries.astype(BF), grad_keys.astype(BF), grad_values.astype(BF)], 1)


def on_device(
    tokens,
    skipped,
    cotangent,
    merge_weight,
    merge_bias,
    first_gain,
    first_shift,
    project_in,
    project_out,
    project_bias,
    second_gain,
    second_shift,
    expand_weight,
    expand_bias,
    reduce_weight,
    reduce_bias,
):
    whole = (
        lax.all_gather(merge_weight, "dp", axis=0, tiled=True),
        lax.all_gather(project_in, "dp", axis=0, tiled=True),
        lax.all_gather(project_out, "dp", axis=0, tiled=True),
        lax.all_gather(expand_weight, "dp", axis=0, tiled=True),
        lax.all_gather(reduce_weight, "dp", axis=0, tiled=True),
        lax.all_gather(merge_bias, "dp", axis=0, tiled=True),
        lax.all_gather(first_gain, "dp", axis=0, tiled=True),
        lax.all_gather(first_shift, "dp", axis=0, tiled=True),
        lax.all_gather(project_bias, "dp", axis=0, tiled=True),
        lax.all_gather(second_gain, "dp", axis=0, tiled=True),
        lax.all_gather(second_shift, "dp", axis=0, tiled=True),
        lax.all_gather(expand_bias, "dp", axis=0, tiled=True),
        lax.all_gather(reduce_bias, "dp", axis=0, tiled=True),
    )
    rows = tokens.shape[0]
    width = tokens.shape[1]
    merge_full, inproj_full, outproj_full, expand_full, reduce_full = (
        whole[0],
        whole[1],
        whole[2],
        whole[3],
        whole[4],
    )
    small = [item.astype(FL) for item in whole[5:]]
    (
        merge_offset,
        gain_one,
        shift_one,
        proj_offset,
        gain_two,
        shift_two,
        expand_offset,
        reduce_offset,
    ) = small
    joined = jnp.concatenate([tokens, skipped], axis=1)
    stream = jnp.dot(joined, merge_full, preferred_element_type=FL) + merge_offset
    normed_one = norm_apply(stream, gain_one, shift_one).astype(BF)
    triple = (
        jnp.dot(normed_one, inproj_full, preferred_element_type=FL)
        .astype(BF)
        .reshape(rows, 3, width)
    )
    heads_side = lax.all_to_all(triple, "seq", split_axis=2, concat_axis=0, tiled=True)
    group = heads_side.shape[0]
    local_width = heads_side.shape[2]
    head_count = local_width // HD
    seq_count = group // LEN
    queries = heads_side[:, 0].reshape(seq_count, LEN, head_count, HD)
    key_rows = heads_side[:, 1].reshape(seq_count, LEN, head_count, HD)
    values = heads_side[:, 2].reshape(seq_count, LEN, head_count, HD)
    mixed, logsum = lax.map(attend_forward, (queries, key_rows, values))
    attended = lax.all_to_all(
        mixed.reshape(group, local_width), "seq", split_axis=0, concat_axis=1, tiled=True
    )
    stream_two = stream + jnp.dot(attended, outproj_full, preferred_element_type=FL) + proj_offset
    normed_two = norm_apply(stream_two, gain_two, shift_two).astype(BF)
    hidden_pre = jnp.dot(normed_two, expand_full, preferred_element_type=FL) + expand_offset
    activated = jax.nn.gelu(hidden_pre, approximate=False).astype(BF)
    mlp_out = jnp.dot(activated, reduce_full, preferred_element_type=FL) + reduce_offset
    output = (stream_two + mlp_out).astype(BF)
    again = (
        lax.all_gather(merge_weight, "dp", axis=0, tiled=True),
        lax.all_gather(project_in, "dp", axis=0, tiled=True),
        lax.all_gather(project_out, "dp", axis=0, tiled=True),
        lax.all_gather(expand_weight, "dp", axis=0, tiled=True),
        lax.all_gather(reduce_weight, "dp", axis=0, tiled=True),
        lax.all_gather(merge_bias, "dp", axis=0, tiled=True),
        lax.all_gather(first_gain, "dp", axis=0, tiled=True),
        lax.all_gather(first_shift, "dp", axis=0, tiled=True),
        lax.all_gather(project_bias, "dp", axis=0, tiled=True),
        lax.all_gather(second_gain, "dp", axis=0, tiled=True),
        lax.all_gather(second_shift, "dp", axis=0, tiled=True),
        lax.all_gather(expand_bias, "dp", axis=0, tiled=True),
        lax.all_gather(reduce_bias, "dp", axis=0, tiled=True),
    )
    merge_back, inproj_back, outproj_back, expand_back, reduce_back = (
        again[0],
        again[1],
        again[2],
        again[3],
        again[4],
    )
    back_small = [item.astype(FL) for item in again[5:]]
    gain_one_back, shift_one_back = (back_small[1], back_small[2])
    gain_two_back, shift_two_back = (back_small[4], back_small[5])
    grad_out = cotangent.astype(FL)
    reduce_weight_grad = jnp.einsum("tf,td->fd", activated, cotangent, preferred_element_type=FL)
    reduce_bias_grad = jnp.sum(grad_out, 0)
    grad_act = jnp.einsum("td,fd->tf", cotangent, reduce_back, preferred_element_type=FL)
    _, gelu_back = jax.vjp(partial(jax.nn.gelu, approximate=False), hidden_pre)
    grad_pre = gelu_back(grad_act)[0].astype(BF)
    expand_weight_grad = jnp.einsum("td,tf->df", normed_two, grad_pre, preferred_element_type=FL)
    expand_bias_grad = jnp.sum(grad_pre.astype(FL), 0)
    grad_normed_two = jnp.einsum("tf,df->td", grad_pre, expand_back, preferred_element_type=FL)
    _, second_back = jax.vjp(norm_apply, stream_two, gain_two_back, shift_two_back)
    grad_rows_two, second_gain_grad, second_shift_grad = second_back(grad_normed_two)
    grad_stream_two = grad_out + grad_rows_two
    grad_branch = grad_stream_two.astype(BF)
    project_out_grad = jnp.einsum("td,te->de", attended, grad_branch, preferred_element_type=FL)
    project_bias_grad = jnp.sum(grad_branch.astype(FL), 0)
    grad_attended = jnp.einsum(
        "te,de->td", grad_branch, outproj_back, preferred_element_type=FL
    ).astype(BF)
    grad_heads = lax.all_to_all(grad_attended, "seq", split_axis=1, concat_axis=0, tiled=True)
    grad_heads = grad_heads.reshape(seq_count, LEN, head_count, HD)
    grad_blocks = lax.map(attend_backward, (queries, key_rows, values, grad_heads, logsum))
    grad_triple = lax.all_to_all(
        grad_blocks.reshape(group, 3, local_width), "seq", split_axis=0, concat_axis=2, tiled=True
    )
    grad_triple = grad_triple.reshape(rows, 3 * width)
    project_in_grad = jnp.einsum("td,te->de", normed_one, grad_triple, preferred_element_type=FL)
    grad_normed_one = jnp.einsum("te,de->td", grad_triple, inproj_back, preferred_element_type=FL)
    _, first_back = jax.vjp(norm_apply, stream, gain_one_back, shift_one_back)
    grad_rows_one, first_gain_grad, first_shift_grad = first_back(grad_normed_one)
    grad_stream = (grad_stream_two + grad_rows_one).astype(BF)
    merge_weight_grad = jnp.einsum("tc,td->cd", joined, grad_stream, preferred_element_type=FL)
    merge_bias_grad = jnp.sum(grad_stream.astype(FL), 0)
    grad_joined = jnp.einsum("td,cd->tc", grad_stream, merge_back, preferred_element_type=FL)
    tokens_grad = grad_joined[:, :width]
    skipped_grad = grad_joined[:, width:]
    reduced = (
        lax.psum_scatter(merge_weight_grad, "dp", scatter_dimension=0, tiled=True),
        lax.psum_scatter(project_in_grad, "dp", scatter_dimension=0, tiled=True),
        lax.psum_scatter(project_out_grad, "dp", scatter_dimension=0, tiled=True),
        lax.psum_scatter(expand_weight_grad, "dp", scatter_dimension=0, tiled=True),
        lax.psum_scatter(reduce_weight_grad, "dp", scatter_dimension=0, tiled=True),
        lax.psum_scatter(merge_bias_grad, "dp", scatter_dimension=0, tiled=True),
        lax.psum_scatter(first_gain_grad, "dp", scatter_dimension=0, tiled=True),
        lax.psum_scatter(first_shift_grad, "dp", scatter_dimension=0, tiled=True),
        lax.psum_scatter(project_bias_grad, "dp", scatter_dimension=0, tiled=True),
        lax.psum_scatter(second_gain_grad, "dp", scatter_dimension=0, tiled=True),
        lax.psum_scatter(second_shift_grad, "dp", scatter_dimension=0, tiled=True),
        lax.psum_scatter(expand_bias_grad, "dp", scatter_dimension=0, tiled=True),
        lax.psum_scatter(reduce_bias_grad, "dp", scatter_dimension=0, tiled=True),
    )
    summed = lax.psum(
        (
            reduced[0],
            reduced[1],
            reduced[2],
            reduced[3],
            reduced[4],
            reduced[5],
            reduced[6],
            reduced[7],
            reduced[8],
            reduced[9],
            reduced[10],
            reduced[11],
            reduced[12],
        ),
        "seq",
    )
    return (
        output,
        tokens_grad,
        skipped_grad,
        summed[0],
        summed[1],
        summed[2],
        summed[3],
        summed[4],
        summed[5],
        summed[6],
        summed[7],
        summed[8],
        summed[9],
        summed[10],
        summed[11],
        summed[12],
    )


def solution(mesh):
    return jax.shard_map(
        on_device,
        mesh=mesh,
        in_specs=(
            P(("dp", "seq"), None),
            P(("dp", "seq"), None),
            P(("dp", "seq"), None),
            P("dp", None),
            P("dp"),
            P("dp"),
            P("dp"),
            P("dp", None),
            P("dp", None),
            P("dp"),
            P("dp"),
            P("dp"),
            P("dp", None),
            P("dp"),
            P("dp", None),
            P("dp"),
        ),
        out_specs=(
            P(("dp", "seq"), None),
            P(("dp", "seq"), None),
            P(("dp", "seq"), None),
            P("dp", None),
            P("dp", None),
            P("dp", None),
            P("dp", None),
            P("dp", None),
            P("dp"),
            P("dp"),
            P("dp"),
            P("dp"),
            P("dp"),
            P("dp"),
            P("dp"),
            P("dp"),
        ),
        check_vma=False,
    )
```

profile of v0, /device:TPU:0, one launch (start us, length us, event | category | flops | bytes accessed | tf_op | source)
XLA Modules:
  0.0 1329.1 jit_solution(1880147046845968387)
XLA Ops:
  17.8 64.3 %all-reduce.18 = (bf16[1024]{0:T(1024)(128)(2,1)S(1)}, bf16[1024]{0:T(1024)(128)(2,1)S(1)}, bf16[1024]{0:T(1024)(128)(2,1)S(1)}, bf16[1024]{0:T(1024)(128)(2,1)S...) all-reduce(bf16[1024]{0:T(1024)(128)(2,1)S(1)} %dynamic-update-slic, ...), channel_id=1, replica_groups=mesh['dp'=16,'seq'=2] {'dp'}, use_global_device_ids=true, to_apply=%add.2 | all-reduce | flops 7168 | bytes 28672
  85.6 5.5 add_reduce_fusion
  92.4 33.6 %all-gather.9.cloned.1.call-done = bf16[1024,3072]{1,0:T(8,128)(2,1)} async-done(((bf16[64,3072]{1,0:T(8,128)(2,1)}), bf16[1024,3072]{1,0:T(8,128)(2,1)}) %all-gather.9.cloned.1.call-update) | async-done | bytes 6291472 | tf_op jit(solution)/shard_map/all_gather | solution.py:72
  126.1 8.3 convolution_convert_fusion
  134.4 6.0 copy.54
  140.4 7.8 copy.55
  148.2 5.9 all-to-all-start
  154.7 58.7 %all-to-all-done = bf16[552,3,1024]{0,1,2:T(4,128)(2,1)} async-done(((bf16[552,3,1024]{0,1,2:T(4,128)(2,1)}), bf16[552,3,1024]{0,1,2:T(4,128)(2,1)}, u32[]{:S(2)}, u32[]{:S(2)}) %all-to-all-start) | async-done | bytes 3391520 | tf_op jit(solution)/shard_map/all_to_all | solution.py:113
  213.5 14.8 %copy.78 = bf16[552,3,2,512]{3,2,0,1:T(2,128)(2,1)S(1)} copy(bf16[552,3,2,512]{0,1,3,2:T(4,128)(2,1)} %bitcast.2) | data formatting | bytes 6782976 | tf_op jit(solution)/shard_map/all_to_all | solution.py:113
  233.7 16.1 %fusion.32 = (f32[8,1104]{1,0:T(8,128)S(1)}, f32[8,1104,1104]{1,2,0:T(8,128)}) fusion(bf16[1104,8,64]{0,2,1:T(8,128)(2,1)S(1)} %bitcast.72, bf16[1104,8,64]{0,2,1:T(8,128)(2,1)S(1)} %bitcast.75), kind=kOutput, calls=%fused_computation.81 | convolution fusion | flops 1267559808 | bytes 41298432 | tf_op jit(solution)/shard_map/while/body/eval_jaxpr/qhd,khd->hqk/dot_general | solution.py:26
  249.8 16.5 %fusion = f32[8,1104]{1,0:T(8,128)S(1)} fusion(f32[8,1104,1104]{1,2,0:T(8,128)} %get-tuple-element.111, f32[8,1104]{1,0:T(8,128)S(1)} %get-tuple-element.110), kind=kLoop, calls=%fused_computation.6 | loop fusion | flops 19492224 | bytes 39072768 | tf_op jit(solution)/shard_map/while/body/eval_jaxpr/reduce_sum | solution.py:29
  267.0 17.8 %fusion.18 = bf16[1104,8,64]{0,2,1:T(8,128)(2,1)} fusion(bf16[1104,8,64]{0,2,1:T(8,128)(2,1)S(1)} %bitcast.80, f32[8,1104,1104]{1,2,0:T(8,128)} %get-tuple-element.111, f32[8,1104]{1,0:T(8,128)S(1)} %fusion, f32[8,1104]{1,0:T(8,128)S(1)} %get-tuple-element.110), kind=kOutput, calls=%fused_computation.41 | convolution fusion | flops 1277884416 | bytes 41333760 | tf_op jit(solution)/shard_map/while/body/eval_jaxpr/hqk,khd->qhd/dot_general | solution.py:31
  291.2 3.6 all-to-all-start.1
  294.9 18.8 %all-gather = bf16[16,1,256]{2,1,0:T(2,128)(2,1)S(1)} all-gather(bf16[1,1,256]{2,1,0:T(2,128)(2,1)S(1)} %reshape.169), channel_id=1, replica_groups=mesh['dp'=16,'seq'=2] {'dp'}, dimensions={0}, use_global_device_ids=true | all-gather | bytes 8704 | tf_op jit(solution)/shard_map/all_gather | solution.py:82
  314.0 4.1 fusion.33
  318.6 11.4 fusion.23
  330.0 30.3 %convert_reduce_fusion = (f32[4096]{0:T(1024)}, bf16[552,4096]{1,0:T(8,128)(2,1)S(1)}, f32[552,4096]{1,0:T(8,128)}) fusion(f32[552,4096]{1,0:T(8,128)} %fusion.23, f32[4096]{0:T(1024)S(1)} %bitcast.91, bf16[552,1024]{1,0:T(8,128)(2,1)S(1)} %copy-done.10, bf16[4096,1024]{1,0:T(8,128)(2,1)} %all-gather.15.cloned.1.call-done), kind=kOutput, calls=%fused_computation.13 | convolution fusion | flops 4800081920 | bytes 32161792 | tf_op jit(solution)/shard_map/td,fd->tf/dot_general | solution.py:159
  360.3 5.8 multiply_reduce_fusion.1
  372.7 3.6 all-to-all-start.2
  376.4 5.5 fusion.36
  382.0 9.8 all-to-all-done.2
  397.8 17.3 %fusion.14 = bf16[8,64,1104]{2,1,0:T(8,128)(2,1)} fusion(bf16[1104,8,64]{0,2,1:T(8,128)(2,1)S(1)} %squeeze.31, f32[8,1104,1104]{1,2,0:T(8,128)} %get-tuple-element.111, f32[8,1104]{1,0:T(8,128)S(1)} %log_add_fusion), kind=kOutput, calls=%fused_computation.37 | convolution fusion | flops 1268133888 | bytes 41298432 | tf_op jit(solution)/shard_map/while/body/eval_jaxpr/hqk,qhd->khd/dot_general | solution.py:41
  415.0 30.2 %multiply_reduce_fusion = (f32[8,1104]{1,0:T(8,128)S(1)}, f32[8,1104,1104]{1,2,0:T(8,128)}) fusion(f32[8,1104,1104]{1,2,0:T(8,128)} %get-tuple-element.111, f32[8,1104]{1,0:T(8,128)S(1)} %log_add_fusion, bf16[1104,8,64]{0,2,1:T(8,128)(2,1)S(1)} %squeeze.31, bf16[1104,8,64]{0,2,1:T(8,128)(2,1)} %bitcast.81), kind=kOutput, calls=%fused_computation.2 | convolution fusion | flops 1277310336 | bytes 80335872 | tf_op jit(solution)/shard_map/while/body/eval_jaxpr/qhd,khd->hqk/dot_general | solution.py:42
  445.3 6.3 copy.71
  451.6 33.2 %multiply_convert_fusion = bf16[8,1104,1104]{1,2,0:T(8,128)(2,1)} fusion(f32[8,1104,1104]{1,2,0:T(8,128)} %get-tuple-element.116, f32[8,1104,1104]{1,2,0:T(8,128)} %get-tuple-element.111, f32[8,1104]{1,0:T(8,128)S(1)} %get-tuple-element.115, f32[8,1104]{1,0:T(8,128)S(1)} %log_add_fusion), kind=kLoop, calls=%fused_computation.1 | loop fusion | flops 39002112 | bytes 97575936 | tf_op jit(solution)/shard_map/while/body/eval_jaxpr/convert_element_type | solution.py:44
  484.8 11.0 fusion.13
  495.8 6.4 copy.70
  502.2 11.2 fusion.12
  513.4 6.3 copy.69
  519.7 9.6 pad_maximum_fusion
  529.3 53.6 %all_to_all.68 = bf16[1104,3,512]{2,1,0:T(4,128)(2,1)S(1)} all-to-all(bf16[1104,3,512]{2,1,0:T(4,128)(2,1)S(1)} %pad_maximum_fusion), channel_id=1, replica_groups=mesh['dp'=16,'seq'=2] {'seq'}, dimensions={0} | all-to-all | bytes 6782976 | tf_op jit(solution)/shard_map/all_to_all | solution.py:177
  583.8 4.4 copy.73
  588.2 8.6 reshape.147
  596.8 8.7 multiply_reduce_fusion.2
  608.5 7.4 fusion.35
  617.6 10.8 fusion.24
  630.2 13.3 fusion.22
  644.2 10.8 multiply_convert_fusion.1
  655.0 12.6 fusion.37
  667.9 48.6 %reduce-scatter.6.cloned.1.call-done = f32[128,1024]{1,0:T(8,128)} async-done(((f32[2048,1024]{1,0:T(8,128)}), f32[128,1024]{1,0:T(8,128)}) %reduce-scatter.6.cloned.1.call-update) | async-done | bytes 524304 | tf_op jit(solution)/shard_map/reduce_scatter | solution.py:192
  716.5 138.6 %reduce-scatter.8.cloned.1.call-done = f32[64,3072]{1,0:T(8,128)} async-done(((f32[1024,3072]{1,0:T(8,128)}), f32[64,3072]{1,0:T(8,128)}) %reduce-scatter.8.cloned.1.call-update) | async-done | bytes 786448 | tf_op jit(solution)/shard_map/reduce_scatter | solution.py:193
  855.2 180.7 %reduce-scatter.12.cloned.1.call-done = f32[64,4096]{1,0:T(8,128)} async-done(((f32[1024,4096]{1,0:T(8,128)}), f32[64,4096]{1,0:T(8,128)}) %reduce-scatter.12.cloned.1.call-update) | async-done | bytes 1048592 | tf_op jit(solution)/shard_map/reduce_scatter | solution.py:195
  1035.9 180.4 %reduce-scatter.14.cloned.1.call-done = f32[256,1024]{1,0:T(8,128)} async-done(((f32[4096,1024]{1,0:T(8,128)}), f32[256,1024]{1,0:T(8,128)}) %reduce-scatter.14.cloned.1.call-update) | async-done | bytes 1048592 | tf_op jit(solution)/shard_map/reduce_scatter | solution.py:196
  1217.7 10.7 add_convert_fusion.2
  1228.4 59.7 %all-reduce.15 = (f32[1024]{0:T(1024)S(1)}, f32[1024]{0:T(1024)S(1)}, f32[1024]{0:T(1024)S(1)}, f32[1024]{0:T(1024)S(1)}, f32[1024]{0:T(1024)S(1)}, /*index=5*/f...) all-reduce(f32[1024]{0:T(1024)S(1)} %get-tuple-element.94, ...), channel_id=7, replica_groups=mesh['dp'=16,'seq'=2] {'dp'}, use_global_device_ids=true, to_apply=%region_22.23.clone | all-reduce | flops 11264 | bytes 90112
  1288.6 5.8 all-reduce.16
  1294.5 4.7 fusion.34
  1302.0 13.5 %all-reduce.21.cloned.1.call-done = (f32[128,1024]{1,0:T(8,128)}, f32[64,3072]{1,0:T(8,128)}, f32[64,1024]{1,0:T(8,128)}, f32[64,4096]{1,0:T(8,128)}, f32[256,1024]{1,0:T(8,128)}) async-done(((f32[128,1024]{1,0:T(8,128)}, f32[64,3072]{1,0:T(8,128)}, f32[64,1024]{1,0:T(8,128)}, f32[64,4096]{1,0:T(8,128)}, f32[256,1024]{1,0:T(8,128)}), (f32[128,1024]{1,0:T(8,128)}, f32[64,3072]{1,0:T(8,128)}, ...) | async-done | bytes 3670032 | tf_op jit(solution)/shard_map/psum | solution.py:206
  (194 shorter events, 59.3 us)
Async XLA Ops:
  7.2 77.3 %copy-start.14 = (bf16[552,1024]{1,0:T(8,128)(2,1)S(1)}, bf16[552,1024]{1,0:T(8,128)(2,1)}, u32[]{:S(2)}) copy-start(bf16[552,1024]{1,0:T(8,128)(2,1)} %param.17) | copy-start | bytes 3391492
  7.2 78.4 %all-gather.7.cloned.1.call-start = ((), (), s32[]{:S(2)}) async-start(), calls=%async_computation.9 | async-start | bytes 4456448 | tf_op jit(solution)/shard_map/all_gather | solution.py:71
  7.9 118.1 %all-gather.9.cloned.1.call-start = ((), (), s32[]{:S(2)}) async-start(), calls=%async_computation.10 | async-start | bytes 6684672 | tf_op jit(solution)/shard_map/all_gather | solution.py:72
  8.7 305.3 %all-gather.11.cloned.1.call-start = ((), (), s32[]{:S(2)}) async-start(), calls=%async_computation.11 | async-start | bytes 2228224 | tf_op jit(solution)/shard_map/all_gather | solution.py:73
  9.4 309.1 %all-gather.13.cloned.1.call-start = ((), (), s32[]{:S(2)}) async-start(), calls=%async_computation.12 | async-start | bytes 8912896 | tf_op jit(solution)/shard_map/all_gather | solution.py:74
  82.2 43.9 %copy-start.38 = (f32[1024]{0:T(1024)}, f32[1024]{0:T(1024)S(1)}, u32[]{:S(2)}) copy-start(f32[1024]{0:T(1024)S(1)} %convert_element_type.107) | copy-start | bytes 12292
  82.2 231.8 %copy-start.28 = (f32[1024]{0:T(1024)}, f32[1024]{0:T(1024)S(1)}, u32[]{:S(2)}) copy-start(f32[1024]{0:T(1024)S(1)} %convert_element_type.105) | copy-start | bytes 12292
  82.2 43.9 %copy-start.33 = (f32[1024]{0:T(1024)}, f32[1024]{0:T(1024)S(1)}, u32[]{:S(2)}) copy-start(f32[1024]{0:T(1024)S(1)} %convert_element_type.106) | copy-start | bytes 12292
  91.1 43.3 %copy-start.6 = (f32[552,1024]{1,0:T(8,128)}, f32[552,1024]{1,0:T(8,128)S(1)}, u32[]{:S(2)}) copy-start(f32[552,1024]{1,0:T(8,128)S(1)} %get-tuple-element.109) | copy-start | bytes 6782980
  91.1 43.3 %copy-start.30 = (f32[552]{0:T(1024)}, f32[552]{0:T(1024)S(1)}, u32[]{:S(2)}) copy-start(f32[552]{0:T(1024)S(1)} %broadcast_multiply_fusion.1) | copy-start | bytes 6628
  92.4 42.0 %copy-start.35 = (f32[552]{0:T(1024)}, f32[552]{0:T(1024)S(1)}, u32[]{:S(2)}) copy-start(f32[552]{0:T(1024)S(1)} %fusion.20) | copy-start | bytes 6628
  148.2 65.3 %all-to-all-start = ((bf16[552,3,1024]{0,1,2:T(4,128)(2,1)}), bf16[552,3,1024]{0,1,2:T(4,128)(2,1)}, u32[]{:S(2)}, u32[]{:S(2)}) async-start(bf16[552,3,1024]{0,1,2:T(4,128)(2,1)} %copy.55), calls=%async_computation | async-start | bytes 10485760 | tf_op jit(solution)/shard_map/all_to_all | solution.py:113
  154.2 175.8 %all-gather.15.cloned.1.call-start = ((), (), s32[]{:S(2)}) async-start(), calls=%async_computation.13 | async-start | bytes 8912896 | tf_op jit(solution)/shard_map/all_gather | solution.py:75
  231.6 18.2 %copy-start = (bf16[1104,1,512]{0,2,1:T(8,128)(2,1)}, bf16[1104,1,512]{0,2,1:T(8,128)(2,1)S(1)}, u32[]{:S(2)}) copy-start(bf16[1104,1,512]{0,2,1:T(8,128)(2,1)S(1)} %copy.59) | copy-start | bytes 3391492
  233.7 32.7 %copy-start.9 = (bf16[1104,1,512]{0,2,1:T(8,128)(2,1)}, bf16[1104,1,512]{0,2,1:T(8,128)(2,1)S(1)}, u32[]{:S(2)}) copy-start(bf16[1104,1,512]{0,2,1:T(8,128)(2,1)S(1)} %copy.58) | copy-start | bytes 3391492
  249.8 16.6 %copy-start.19 = (f32[8,1104]{1,0:T(8,128)}, f32[8,1104]{1,0:T(8,128)S(1)}, u32[]{:S(2)}) copy-start(f32[8,1104]{1,0:T(8,128)S(1)} %get-tuple-element.110) | copy-start | bytes 105988
  288.1 6.7 copy-start.47
  291.2 22.5 %all-to-all-start.1 = ((bf16[2,552,512]{2,1,0:T(8,128)(2,1)}), bf16[2,552,512]{2,1,0:T(8,128)(2,1)S(1)}, u32[]{:S(2)}, u32[]{:S(2)}) async-start(bf16[2,552,512]{2,1,0:T(8,128)(2,1)} %copy.62), calls=%async_computation.1 | async-start | bytes 2260992 | tf_op jit(solution)/shard_map/all_to_all | solution.py:122
  294.9 23.7 %copy-start.40 = (f32[1024]{0:T(1024)}, f32[1024]{0:T(1024)S(1)}, u32[]{:S(2)}) copy-start(f32[1024]{0:T(1024)S(1)} %convert_element_type.115) | copy-start | bytes 12292
  313.7 16.3 %copy-start.24 = (f32[16,1,256]{2,1,0:T(1,128)}, f32[16,1,256]{2,1,0:T(1,128)S(1)}, u32[]{:S(2)}) copy-start(f32[16,1,256]{2,1,0:T(1,128)S(1)} %convert_element_type.137) | copy-start | bytes 49156
  318.1 42.2 %copy-start.4 = (f32[552,1024]{1,0:T(8,128)}, f32[552,1024]{1,0:T(8,128)S(1)}, u32[]{:S(2)}) copy-start(f32[552,1024]{1,0:T(8,128)S(1)} %get-tuple-element.113) | copy-start | bytes 6782980
  318.5 11.5 copy-start.10
  330.0 30.4 %copy-start.45 = (bf16[1024,4096]{1,0:T(8,128)(2,1)S(1)}, bf16[1024,4096]{1,0:T(8,128)(2,1)}, u32[]{:S(2)}) copy-start(bf16[1024,4096]{1,0:T(8,128)(2,1)} %all-gather.13.cloned.1.call-done) | copy-start | bytes 25165828
  360.3 5.8 copy-start.48
  371.6 4.8 copy-start.20
  371.6 4.8 copy-start.23
  372.7 19.0 %all-to-all-start.2 = ((bf16[552,2,512]{2,0,1:T(8,128)(2,1)}), bf16[552,2,512]{2,0,1:T(8,128)(2,1)S(1)}, u32[]{:S(2)}, u32[]{:S(2)}) async-start(bf16[552,2,512]{2,0,1:T(8,128)(2,1)} %bitcast.86), calls=%async_computation.2 | async-start | bytes 2260992 | tf_op jit(solution)/shard_map/all_to_all | solution.py:174
  376.3 291.6 %reduce-scatter.10.cloned.1.call-start = ((), (), s32[]{:S(2)}) async-start(), calls=%async_computation.16 | async-start | bytes 4456448 | tf_op jit(solution)/shard_map/reduce_scatter | solution.py:194
  381.9 334.6 %reduce-scatter.6.cloned.1.call-start = ((), (), s32[]{:S(2)}) async-start(), calls=%async_computation.14 | async-start | bytes 8912896 | tf_op jit(solution)/shard_map/reduce_scatter | solution.py:192
  451.6 33.2 %copy-start.1 = (bf16[1104,1,512]{0,2,1:T(8,128)(2,1)S(1)}, bf16[1104,1,512]{0,2,1:T(8,128)(2,1)}, u32[]{:S(2)}) copy-start(bf16[1104,1,512]{0,2,1:T(8,128)(2,1)} %copy-done) | copy-start | bytes 3391492
  495.8 6.4 copy-start.3
  588.2 8.6 copy-start.29
  588.2 8.6 copy-start.31
  588.2 8.6 copy-start.34
  588.2 8.6 copy-start.36
  596.8 8.7 copy-start.27
  596.8 8.8 copy-start.7
  615.9 239.2 %reduce-scatter.8.cloned.1.call-start = ((), (), s32[]{:S(2)}) async-start(), calls=%async_computation.15 | async-start | bytes 13369344 | tf_op jit(solution)/shard_map/reduce_scatter | solution.py:193
  628.4 407.5 %reduce-scatter.12.cloned.1.call-start = ((), (), s32[]{:S(2)}) async-start(), calls=%async_computation.17 | async-start | bytes 17825792 | tf_op jit(solution)/shard_map/reduce_scatter | solution.py:195
  643.5 572.8 %reduce-scatter.14.cloned.1.call-start = ((), (), s32[]{:S(2)}) async-start(), calls=%async_computation.18 | async-start | bytes 17825792 | tf_op jit(solution)/shard_map/reduce_scatter | solution.py:196
  667.6 550.0 %copy-start.44 = (bf16[1024]{0:T(1024)(128)(2,1)S(1)}, bf16[1024]{0:T(1024)(128)(2,1)}, u32[]{:S(2)}) copy-start(bf16[1024]{0:T(1024)(128)(2,1)} %get-tuple-element.88) | copy-start | bytes 6148
  667.6 647.9 %all-reduce.21.cloned.1.call-start = ((), (), s32[]{:S(2)}) async-start(), calls=%async_computation.19 | async-start | bytes 7340032 | tf_op jit(solution)/shard_map/psum | solution.py:206
  1217.6 10.7 copy-start.32
  1217.7 10.7 copy-start.37
  1217.7 10.7 copy-start.42
  1217.7 10.7 copy-start.43
  1217.7 76.8 %copy-start.13 = (bf16[552,1024]{1,0:T(8,128)(2,1)S(1)}, bf16[552,1024]{1,0:T(8,128)(2,1)}, u32[]{:S(2)}) copy-start(bf16[552,1024]{1,0:T(8,128)(2,1)} %copy-done.12) | copy-start | bytes 3391492
  1315.5 4.9 copy-start.18
  (15 other events, 30.1 us)
Sparse Core Ops, SparseCore 0:
  10.2 53.5 all-gather.6
  66.1 59.9 all-gather.8
  128.2 40.1 all-gather.10
  170.4 73.0 all-gather.12
  245.5 73.0 all-gather.14
  382.0 71.0 reduce-scatter.9
  616.1 100.4 reduce-scatter.5
  720.6 134.5 reduce-scatter.7
  859.3 176.5 reduce-scatter.11
  1039.9 176.4 reduce-scatter.13
  1218.9 96.5 all-reduce.20
where the time goes:
time: 1340 us; the launch traced here: 1330 us
  waiting for transfers between devices  667 us (50%)
  matrix products  244 us (18%)
  blocking collectives  202 us (15%)
  local copies, waits for them, and re-layouts  109 us (8%)
  other arithmetic  75.9 us (6%)
  between operations  16.7 us (1%)
  starting transfers between devices  14 us (1%)
    reduce_scatter x1, waiting for transfers between devices, on_device(): lax.psum_scatter(expand_weight_grad, 'dp', scatter_dimension=0, tiled=True)  181 us
    reduce_scatter x1, waiting for transfers between devices, on_device(): lax.psum_scatter(reduce_weight_grad, 'dp', scatter_dimension=0, tiled=True)  180 us
    reduce_scatter x1, waiting for transfers between devices, on_device(): lax.psum_scatter(project_in_grad, 'dp', scatter_dimension=0, tiled=True)  139 us
    unnamed x2, blocking collectives  124 us
    all_to_all x1, waiting for transfers between devices, on_device(): lax.all_to_all(triple, 'seq', split_axis=2, concat_axis=0, tiled=True)  58.7 us
    all_to_all x1, blocking collectives, on_device(): lax.all_to_all(grad_blocks.reshape(group, 3, local_width), 'seq', split_a...  53.6 us
    reduce_scatter x1, waiting for transfers between devices, on_device(): lax.psum_scatter(merge_weight_grad, 'dp', scatter_dimension=0, tiled=True)  48.6 us
    all_gather x1, waiting for transfers between devices, on_device(): lax.all_gather(project_in, 'dp', axis=0, tiled=True)  33.6 us
  transfers between devices with their start and end apart: 14, of which 8 were waited for; matrix products, arithmetic and copies ran while one was open for 28% of the time, Pallas kernels for 0%

commit v1 on v0

v1 whole, which is shorter than its diff:
```python
import functools
from functools import partial

import jax
import jax.numpy as jnp
from jax import lax
from jax.experimental import pallas as pl
from jax.experimental.pallas import tpu as pltpu
from jax.sharding import PartitionSpec as P

HD = 64
EPSILON = 1e-05
BF = jnp.bfloat16
FL = jnp.float32
MESHID = pl.DeviceIdType.MESH


def gather_kernel(Z, R, rc, L, shard, out, buf, lsem, su, ru, sd, rd, sy, ry, sx, rx, sc, rcv):
    n=R//rc
    hc=rc//2
    dp=lax.axis_index("dp"); s=lax.axis_index("seq")
    c=dp%2; y=(dp//2)%2; z=dp//4; h=s%2
    upd=(dp+4, s); dnd=(dp-4, s)
    yd=(dp+2-4*y, s); xd=(dp, s+1-2*h); cd=(dp+1-2*c, s)
    bar=pltpu.get_barrier_semaphore()
    has_up=z<Z-1; has_dn=z>0
    load=pltpu.make_async_copy(shard, buf, lsem.at[0]); load.start()
    @pl.when(has_up)
    def _(): pl.semaphore_signal(bar,inc=1,device_id=upd,device_id_type=MESHID)
    @pl.when(has_dn)
    def _(): pl.semaphore_signal(bar,inc=1,device_id=dnd,device_id_type=MESHID)
    for t in (yd,xd,cd): pl.semaphore_signal(bar,inc=1,device_id=t,device_id_type=MESHID)
    pl.semaphore_wait(bar,5-(z==0).astype(jnp.int32)-(z==Z-1).astype(jnp.int32))
    load.wait()
    store=pltpu.make_async_copy(buf, out.at[z,y,c], lsem.at[1]); store.start()
    def rows(k): return pl.ds(pl.multiple_of(k*rc,rc),rc)
    def half(k): return pl.ds(pl.multiple_of(k*rc+h*hc,hc),hc)
    def upc(d,k):
        src = buf.at[rows(k)] if d==0 else out.at[z-d,y,c,rows(k)]
        return pltpu.make_async_remote_copy(src, out.at[z-d,y,c,rows(k)], su.at[d,k], ru.at[d,k], device_id=upd, device_id_type=MESHID)
    def dnc(d,k):
        src = buf.at[rows(k)] if d==0 else out.at[z+d,y,c,rows(k)]
        return pltpu.make_async_remote_copy(src, out.at[z+d,y,c,rows(k)], sd.at[d,k], rd.at[d,k], device_id=dnd, device_id_type=MESHID)
    def ycp(k,mine):
        yy=y if mine else 1-y
        r=out.at[:,yy,c,half(k)]
        return pltpu.make_async_remote_copy(r,r,sy.at[k],ry.at[k],device_id=yd,device_id_type=MESHID)
    def xcp(k,mine):
        hh=half(k) if mine else pl.ds(pl.multiple_of(k*rc+(1-h)*hc,hc),hc)
        r=out.at[:,1-y,c,hh]
        return pltpu.make_async_remote_copy(r,r,sx.at[k],rx.at[k],device_id=xd,device_id_type=MESHID)
    def ccp(k,mine):
        r=out.at[:,:,c if mine else 1-c,rows(k)]
        return pltpu.make_async_remote_copy(r,r,sc.at[k],rcv.at[k],device_id=cd,device_id_type=MESHID)
    D=(Z-1)*L
    total=n+D+3*L
    def valid(k): return (k>=0)&(k<n)
    def body(t,_):
        for d in range(Z-1):
            k=t-d*L
            if d>0:
                @pl.when(valid(k)&(z>=d))
                def _():
                    pltpu.make_async_remote_copy(out.at[z-d,y,c,rows(k)],out.at[z-d,y,c,rows(k)],su.at[d-1,k],ru.at[d-1,k],device_id=dnd,device_id_type=MESHID).wait_recv()
                @pl.when(valid(k)&(z+d<=Z-1))
                def _():
                    pltpu.make_async_remote_copy(out.at[z+d,y,c,rows(k)],out.at[z+d,y,c,rows(k)],sd.at[d-1,k],rd.at[d-1,k],device_id=upd,device_id_type=MESHID).wait_recv()
            @pl.when(valid(k)&has_up&(z>=d))
            def _(): upc(d,k).start()
            @pl.when(valid(k)&has_dn&(z+d<=Z-1))
            def _(): dnc(d,k).start()
        d=Z-1
        k=t-D
        @pl.when(valid(k)&(z>=d))
        def _():
            pltpu.make_async_remote_copy(out.at[z-d,y,c,rows(k)],out.at[z-d,y,c,rows(k)],su.at[d-1,k],ru.at[d-1,k],device_id=dnd,device_id_type=MESHID).wait_recv()
        @pl.when(valid(k)&(z+d<=Z-1))
        def _():
            pltpu.make_async_remote_copy(out.at[z+d,y,c,rows(k)],out.at[z+d,y,c,rows(k)],sd.at[d-1,k],rd.at[d-1,k],device_id=upd,device_id_type=MESHID).wait_recv()
        @pl.when(k==0)
        def _(): store.wait()
        @pl.when(valid(k))
        def _(): ycp(k,True).start()
        k1=k-L
        @pl.when(valid(k1))
        def _():
            ycp(k1,False).wait_recv()
            xcp(k1,True).start()
        k2=k-2*L
        @pl.when(valid(k2))
        def _():
            xcp(k2,False).wait_recv()
            ccp(k2,True).start()
        k3=k-3*L
        @pl.when(valid(k3))
        def _(): ccp(k3,False).wait_recv()
        return 0
    lax.fori_loop(0,total,body,0)
    def drain(k,_):
        for d in range(Z-1):
            @pl.when(has_up&(z>=d))
            def _(): upc(d,k).wait_send()
            @pl.when(has_dn&(z+d<=Z-1))
            def _(): dnc(d,k).wait_send()
        ycp(k,True).wait_send(); xcp(k,True).wait_send(); ccp(k,True).wait_send()
        return 0
    lax.fori_loop(0,n,drain,0)

def gather(shard, Z, rc, L, cid):
    R=shard.shape[0]; n=R//rc; W=shard.shape[1]
    S=pltpu.SemaphoreType.DMA
    return pl.pallas_call(functools.partial(gather_kernel,Z,R,rc,L),
        out_shape=jax.ShapeDtypeStruct((Z,2,2,R,W),shard.dtype),
        in_specs=[pl.BlockSpec(memory_space=pl.ANY)], out_specs=pl.BlockSpec(memory_space=pl.ANY),
        scratch_shapes=[pltpu.VMEM((R,W),shard.dtype),S((2,)),S((Z-1,n)),S((Z-1,n)),S((Z-1,n)),S((Z-1,n)),S((n,)),S((n,)),S((n,)),S((n,)),S((n,)),S((n,))],
        compiler_params=pltpu.CompilerParams(collective_id=cid,has_side_effects=True))(shard)


def reduce_kernel(Z, T, L, segs, nx, ny, no, *refs):
    xs=refs[:nx]; ys=refs[nx:nx+ny]; outs=refs[nx+ny:nx+ny+no]
    (xbuf, ybuf, keep, s0, r0, s1, r1, s2, r2, su, ru, sd, rd, sx, rx, own, e_buf,
     xsem, ysem, q0, p0, q1, p1, q2, p2, qu, pu, qd, pd, qx, px) = refs[nx+ny+no:]
    dp=lax.axis_index("dp"); s=lax.axis_index("seq")
    c=dp%2; y=(dp//2)%2; z=dp//4; h=s%2
    upd=(dp+4,s); dnd=(dp-4,s); yd=(dp+2-4*y,s); xd=(dp,s+1-2*h); cd=(dp+1-2*c,s)
    has_up=z<Z-1; has_dn=z>0
    n=sum(g[5] for g in segs)
    starts=[]; a=0
    for g in segs: starts.append(a); a+=g[5]
    def load_x(i):
        xi,pieces,*_=segs[i]
        off=0; res=[]
        for (c0,w) in pieces:
            res.append(pltpu.make_async_copy(xs[xi].at[:,c0:c0+w], xbuf.at[i%2,:,off:off+w], xsem.at[i%2,len(res)])); off+=w
        return res
    def load_y(i,k):
        _,_,yi,c0,wide,cnt,_,_=segs[i]
        w=16384//wide
        return pltpu.make_async_copy(ys[yi].at[:,pl.ds(pl.multiple_of(c0+(k-starts[i])*w,128),w)], ybuf.at[k%2,:,0:w], ysem.at[k%2])
    def each(k,fn):
        for i in range(len(segs)):
            @pl.when((k>=starts[i])&(k<starts[i]+segs[i][5]))
            def _(): fn(i)
    for q in load_x(0): q.start()
    load_y(0,0).start()
    bar=pltpu.get_barrier_semaphore()
    @pl.when(has_up)
    def _(): pl.semaphore_signal(bar,inc=1,device_id=upd,device_id_type=MESHID)
    @pl.when(has_dn)
    def _(): pl.semaphore_signal(bar,inc=1,device_id=dnd,device_id_type=MESHID)
    for t in (yd,xd,cd): pl.semaphore_signal(bar,inc=1,device_id=t,device_id_type=MESHID)
    pl.semaphore_wait(bar,5-(z==0).astype(jnp.int32)-(z==Z-1).astype(jnp.int32))
    def rcopy(src,dst,ss,rs,dev): return pltpu.make_async_remote_copy(src,dst,ss,rs,device_id=dev,device_id_type=MESHID)
    NS=s0.shape[0]
    def c0(k): return rcopy(s0.at[k%NS],r0.at[k],q0.at[k%NS],p0.at[k],cd)
    def c1(k): return rcopy(s1.at[k%NS],r1.at[k],q1.at[k%NS],p1.at[k],xd)
    def c2(k): return rcopy(s2.at[k%NS],r2.at[k],q2.at[k%NS],p2.at[k],yd)
    def cu(k,j): return rcopy(su.at[k%NS,j],ru.at[k,j],qu.at[k%NS,j],pu.at[k,j],upd)
    def cdn(k,j): return rcopy(sd.at[k%NS,j],rd.at[k,j],qd.at[k%NS,j],pd.at[k,j],dnd)
    def cx(k): return rcopy(sx.at[k%NS],rx.at[k],qx.at[k%NS],px.at[k],xd)
    NE=e_buf.shape[0]; NK=keep.shape[0]
    mine=pl.ds(pl.multiple_of(h*32,32),32); other=pl.ds(pl.multiple_of((1-h)*32,32),32)
    def valid(k): return (k>=0)&(k<n)
    B1=L; B2=2*L; B3=3*L; BX=B3+(Z-1)*L+L; BF_=BX+L
    total=n+BF_
    def body(t,_):
        k=t
        @pl.when(valid(k))
        def _():
            def go(i):
                @pl.when(k==starts[i])
                def _():
                    for q in load_x(i): q.wait()
                    if i+1<len(segs):
                        for q in load_x(i+1): q.start()
                load_y(i,k).wait()
                @pl.when(k+1<starts[i]+segs[i][5])
                def _(): load_y(i,k+1).start()
                if i+1<len(segs):
                    @pl.when(k+1==starts[i]+segs[i][5])
                    def _(): load_y(i+1,k+1).start()
            each(k,go)
            @pl.when(k>=NS)
            def _(): c0(k-NS).wait_send()
            def comp(rr,par):
                cw=16384//rr
                r=lax.dot_general(xbuf[par,:,0:4*Z*rr],ybuf[k%2,:,0:cw],(((0,),(0,)),((),())),preferred_element_type=FL)
                r=r.astype(BF).reshape(Z,2,2,rr,cw)
                for cc in range(2):
                    @pl.when(c==cc)
                    def _():
                        for dst,part in ((keep.at[k%NK],r[:,:,cc]),(s0.at[k%NS],r[:,:,1-cc])):
                            if rr==128:
                                dst[:,:,:,0:128]=part[:,:,0:64]
                                dst[:,:,:,128:256]=part[:,:,64:128]
                            elif rr==64:
                                dst[...]=part
                            else:
                                dst[:,:,0:32,:]=part[:,:,:,0:256]
                                dst[:,:,32:64,:]=part[:,:,:,256:512]
            for par in range(2):
                for wide in (32,64,128):
                    conds=[(k>=starts[i])&(k<starts[i]+segs[i][5]) for i in range(len(segs)) if i%2==par and segs[i][4]==wide]
                    if conds:
                        cnd=functools.reduce(lambda a,b:a|b,conds)
                        @pl.when(cnd)
                        def _(): comp(wide,par)
            c0(k).start()
        k1=t-B1
        @pl.when(valid(k1))
        def _():
            c0(k1).wait_recv()
            @pl.when(k1>=NS)
            def _(): c1(k1-NS).wait_send()
            b=keep.at[k1%NK]
            s1[k1%NS]=(b[:,1-y,other,:].astype(FL)+r0[k1,:,1-y,other,:].astype(FL)).astype(BF)
            c1(k1).start()
            b[:,1-y,mine,:]=(b[:,1-y,mine,:].astype(FL)+r0[k1,:,1-y,mine,:].astype(FL)).astype(BF)
            e_buf[k1%NE]=(b[:,y].astype(FL)+r0[k1,:,y].astype(FL)).astype(BF)
        k2=t-B2
        @pl.when(valid(k2))
        def _():
            c1(k2).wait_recv()
            @pl.when(k2>=NS)
            def _(): c2(k2-NS).wait_send()
            s2[k2%NS]=(keep[k2%NK,:,1-y,mine,:].astype(FL)+r1[k2].astype(FL)).astype(BF)
            c2(k2).start()
        k3=t-B3
        @pl.when(valid(k3))
        def _():
            c2(k3).wait_recv()
            e_buf[k3%NE,:,mine,:]=(e_buf[k3%NE,:,mine,:].astype(FL)+r2[k3].astype(FL)).astype(BF)
        ku=t-B3-z*L
        @pl.when(valid(ku))
        def _():
            for j in range(Z):
                @pl.when((z==0)&(j>0))
                def _():
                    @pl.when(ku>=NS)
                    def _(): cu(ku-NS,j).wait_send()
                    su[ku%NS,j]=e_buf[ku%NE,j]
                    cu(ku,j).start()
                @pl.when((z>0)&(z<=j))
                def _(): cu(ku,j).wait_recv()
                @pl.when((z>0)&(z<j))
                def _():
                    @pl.when(ku>=NS)
                    def _(): cu(ku-NS,j).wait_send()
                    su[ku%NS,j]=(e_buf[ku%NE,j].astype(FL)+ru[ku,j].astype(FL)).astype(BF)
                    cu(ku,j).start()
        kd=t-B3-(Z-1-z)*L
        @pl.when(valid(kd))
        def _():
            for j in range(Z):
                @pl.when((z==Z-1)&(j<Z-1))
                def _():
                    @pl.when(kd>=NS)
                    def _(): cdn(kd-NS,j).wait_send()
                    sd[kd%NS,j]=e_buf[kd%NE,j]
                    cdn(kd,j).start()
                @pl.when((z<Z-1)&(z>=j))
                def _(): cdn(kd,j).wait_recv()
                @pl.when((z<Z-1)&(z>j))
                def _():
                    @pl.when(kd>=NS)
                    def _(): cdn(kd-NS,j).wait_send()
                    sd[kd%NS,j]=(e_buf[kd%NE,j].astype(FL)+rd[kd,j].astype(FL)).astype(BF)
                    cdn(kd,j).start()
        kx=t-BX
        @pl.when(valid(kx))
        def _():
            @pl.when(kx>=NS)
            def _(): cx(kx-NS).wait_send()
            for j in range(Z):
                @pl.when(z==j)
                def _():
                    v=e_buf[kx%NE,j].astype(FL)
                    if j>0: v=v+ru[kx,j].astype(FL)
                    if j<Z-1: v=v+rd[kx,j].astype(FL)
                    sx[kx%NS]=v.astype(BF)
            cx(kx).start()
        kf=t-BF_
        @pl.when(valid(kf))
        def _():
            cx(kf).wait_recv()
            v=sx[kf%NS].astype(FL)+rx[kf].astype(FL)
            def put(i):
                _,_,_,_,wide,cnt,oi,r0_=segs[i]
                j=kf-starts[i]
                row,col=r0_
                def cs(at,w): return pl.ds(pl.multiple_of(col+j*(16384//wide)+at,128),w)
                if wide==128:
                    outs[oi][row:row+64,cs(0,128)]=v[:,0:128]
                    outs[oi][row+64:row+128,cs(0,128)]=v[:,128:256]
                elif wide==64:
                    outs[oi][row:row+64,cs(0,256)]=v
                else:
                    outs[oi][row:row+32,cs(0,256)]=v[0:32]
                    outs[oi][row:row+32,cs(256,256)]=v[32:64]
            each(kf,put)
        return 0
    lax.fori_loop(0,total,body,0)
    def drain(k,_):
        c0(k).wait_send(); c1(k).wait_send(); c2(k).wait_send(); cx(k).wait_send()
        for j in range(Z):
            @pl.when(has_up&(z<j))
            def _(): cu(k,j).wait_send()
            @pl.when(has_dn&(z>j))
            def _(): cdn(k,j).wait_send()
        return 0
    lax.fori_loop(max(n-NS,0),n,drain,0)

def reduce_grads(xs, ys, segs, outshapes, Z, L, cid):
    T=xs[0].shape[0]
    n=sum(g[5] for g in segs)
    NS=4; NK=2*L+2; NE=(Z+3)*L+2
    S=pltpu.SemaphoreType.DMA
    V=pltpu.VMEM
    npc=max(len(g[1]) for g in segs)
    xw=max(sum(w for _,w in g[1]) for g in segs); yw=max(16384//g[4] for g in segs)
    scratch=[V((2,T,xw),BF),V((2,T,yw),BF),V((NK,Z,2,64,256),BF),
        V((NS,Z,2,64,256),BF),V((n,Z,2,64,256),BF), V((NS,Z,32,256),BF),V((n,Z,32,256),BF), V((NS,Z,32,256),BF),V((n,Z,32,256),BF),
        V((NS,Z,64,256),BF),V((n,Z,64,256),BF),V((NS,Z,64,256),BF),V((n,Z,64,256),BF),V((NS,64,256),BF),V((n,64,256),BF),V((8,128),FL),V((NE,Z,64,256),BF),
        S((2,npc)),S((2,)),S((NS,)),S((n,)),S((NS,)),S((n,)),S((NS,)),S((n,)),S((NS,Z)),S((n,Z)),S((NS,Z)),S((n,Z)),S((NS,)),S((n,))]
    return pl.pallas_call(functools.partial(reduce_kernel,Z,T,L,segs,len(xs),len(ys),len(outshapes)),
        out_shape=[jax.ShapeDtypeStruct(o,FL) for o in outshapes],
        in_specs=[pl.BlockSpec(memory_space=pl.ANY)]*(len(xs)+len(ys)),
        out_specs=[pl.BlockSpec(memory_space=pltpu.VMEM)]*len(outshapes),
        scratch_shapes=scratch,
        compiler_params=pltpu.CompilerParams(collective_id=cid,has_side_effects=True,vmem_limit_bytes=64*1024*1024-65536))(*xs,*ys)
def segments(xi,yi,oi,dps,rows,xcols,ycols,oc=0):
    rr=min(rows,128)
    res=[]
    for q in range(rows//rr):
        pieces=((0,xcols),) if rr==rows else tuple((d*rows+q*rr,rr) for d in range(dps))
        res.append((xi,pieces,yi,0,rr,ycols*rr//16384,oi,(q*rr,oc)))
    return res


def dot(a,b,ca,cb): return lax.dot_general(a,b,(((ca,),(cb,)),((),())),preferred_element_type=FL)
def fwd_kernel(HD, qr, ko, kt, vo, vt, o_ref, lse_ref):
    lane=lax.broadcasted_iota(jnp.int32,(1,128),1)
    first=lane<HD
    q=qr[...]*jnp.asarray(HD**-0.5,BF)
    k=jnp.concatenate([ko[...],kt[...]],0); v=jnp.concatenate([vo[...],vt[...]],0)
    res=[]
    for hd in range(2):
        m=first if hd==0 else ~first
        qm=jnp.where(m,q,jnp.zeros_like(q))
        s=dot(qm,k,1,1)
        mx=jnp.max(s,-1,keepdims=True)
        p=jnp.exp(s-mx)
        l=jnp.sum(p,-1,keepdims=True)
        o=dot(p.astype(BF),v,1,0)/l
        res.append((o,mx+jnp.log(l)))
    o_ref[...]=jnp.where(first,res[0][0],res[1][0]).astype(BF)
    lse_ref[...]=jnp.where(first,res[0][1],res[1][1])
def att_fwd(q,ko,kt,vo,vt,HD=64):
    T,D=q.shape
    spec=pl.BlockSpec((T,128),lambda i:(0,i))
    return pl.pallas_call(functools.partial(fwd_kernel,HD),grid=(D//128,),in_specs=[spec]*5,out_specs=[spec,spec],
        out_shape=[jax.ShapeDtypeStruct((T,D),BF),jax.ShapeDtypeStruct((T,D),FL)],
        compiler_params=pltpu.CompilerParams(vmem_limit_bytes=56*1024*1024))(q,ko,kt,vo,vt)
def bwd_kernel(HD, qr, ko, kt, vo, vt, o_ref, lse_ref, g_ref, dq_ref, dko, dkt, dvo, dvt):
    T=qr.shape[0]
    lane=lax.broadcasted_iota(jnp.int32,(1,128),1)
    first=lane<HD
    sc=HD**-0.5
    q=qr[...]*jnp.asarray(sc,BF)
    k=jnp.concatenate([ko[...],kt[...]],0); v=jnp.concatenate([vo[...],vt[...]],0)
    g=g_ref[...]
    go=g.astype(FL)*o_ref[...].astype(FL)
    lse=lse_ref[...]
    dqs=[]; dk=None
    for hd in range(2):
        m=first if hd==0 else ~first
        qm=jnp.where(m,q,jnp.zeros_like(q)); gm=jnp.where(m,g,jnp.zeros_like(g))
        delta=jnp.sum(jnp.where(m,go,0.0),-1,keepdims=True)
        ls=lse[:,hd*HD:hd*HD+1]
        s=dot(qm,k,1,1)
        p=jnp.exp(s-ls)
        dp=dot(gm,v,1,1)
        ds=(p*(dp-delta)).astype(BF)
        pb=p.astype(BF)
        dvv=dot(pb,gm,0,0)
        dkk=dot(ds,qm,0,0)
        dqs.append(dot(ds,k,1,0))
        if dk is None: dk,dv=dkk,dvv
        else: dk=dk+dkk; dv=dv+dvv
    dq_ref[...]=(jnp.where(first,dqs[0],dqs[1])*sc).astype(BF)
    dko[...]=dk[:T]; dkt[...]=dk[T:].astype(BF)
    dvo[...]=dv[:T]; dvt[...]=dv[T:].astype(BF)
def att_bwd(q,ko,kt,vo,vt,o,lse,g,HD=64):
    T,D=q.shape
    spec=pl.BlockSpec((T,128),lambda i:(0,i))
    return pl.pallas_call(functools.partial(bwd_kernel,HD),grid=(D//128,),in_specs=[spec]*8,out_specs=[spec]*5,
        out_shape=[jax.ShapeDtypeStruct((T,D),t) for t in (BF,FL,BF,FL,BF)],
        compiler_params=pltpu.CompilerParams(vmem_limit_bytes=60*1024*1024))(q,ko,kt,vo,vt,o,lse,g)


def norm_apply(stream, gain, shift):
    centred = stream - jnp.mean(stream, -1, keepdims=True)
    variance = jnp.mean(centred * centred, -1, keepdims=True)
    return centred * lax.rsqrt(variance + EPSILON) * gain + shift


def mm(left, right):
    return jnp.dot(left, right, preferred_element_type=FL)


def mmt(left, right):
    return lax.dot_general(left, right, (((1,), (1,)), ((), ())), preferred_element_type=FL)


def on_device(
    dps,
    seqs,
    tokens,
    skipped,
    cotangent,
    merge_weight,
    merge_bias,
    first_gain,
    first_shift,
    project_in,
    project_out,
    project_bias,
    second_gain,
    second_shift,
    expand_weight,
    expand_bias,
    reduce_weight,
    reduce_bias,
):
    rows, width = tokens.shape
    depth = dps // 4
    hidden = expand_weight.shape[1]
    dp = lax.axis_index("dp")
    seq = lax.axis_index("seq")
    cross = []
    pair = []
    for d in range(dps):
        for s in range(seqs):
            if d % 2 != s % 2:
                cross.append((d * seqs + s, (d + (1 if s % 2 else -1)) * seqs + s + (1 if d % 2 else -1)))
            pair.append((d * seqs + s, (d ^ 1) * seqs + s))
    stays = (dp % 2) == (seq % 2)

    def swap(value):
        return jnp.where(stays, value, lax.ppermute(value, ("dp", "seq"), cross))

    def other_core(value):
        return lax.ppermute(value, ("dp", "seq"), pair)

    own_tokens, own_skipped, own_cot = tokens, skipped, cotangent
    tokens, skipped, cotangent = swap(tokens), swap(skipped), swap(cotangent)

    small_list = [merge_bias, first_gain, first_shift, project_bias, second_gain, second_shift, reduce_bias, expand_bias]
    small = jnp.concatenate(small_list)
    piece = merge_bias.shape[0]
    small = jnp.pad(small.reshape(1, -1), ((0, 31), (0, width - small.shape[0])))
    cols = lambda w: [w[:, i * width : (i + 1) * width] for i in range(w.shape[1] // width)]
    parts = [merge_weight, *cols(project_in), small, project_out, *cols(expand_weight), reduce_weight]
    shard = jnp.concatenate(parts, 0)
    bounds = [0]
    for p in parts:
        bounds.append(bounds[-1] + p.shape[0])
    gathered = gather(shard, depth, 32, 1, 0).reshape(dps, shard.shape[0], width)

    def whole(i):
        return gathered[:, bounds[i] : bounds[i + 1]].reshape(-1, width)

    merge_full = whole(0)
    w_q, w_k, w_v = whole(1), whole(2), whole(3)
    out_full = whole(5)
    w_exp = [whole(6 + i) for i in range(hidden // width)]
    reduce_full = whole(6 + hidden // width)
    sm = gathered[:, bounds[4]].astype(FL)
    vec = [sm[:, i * piece : (i + 1) * piece].reshape(-1) for i in range(7)]
    merge_offset, gain_one, shift_one, proj_offset, gain_two, shift_two, reduce_offset = vec
    expand_offset = sm[:, 7 * piece : 7 * piece + hidden // dps].reshape(-1)

    joined = jnp.concatenate([tokens, skipped], axis=1)
    stream = mm(joined, merge_full) + merge_offset
    normed_one = norm_apply(stream, gain_one, shift_one).astype(BF)
    keys = mm(normed_one, w_k).astype(BF)
    values = mm(normed_one, w_v).astype(BF)
    keys_t, values_t = other_core(keys), other_core(values)
    queries = mm(normed_one, w_q).astype(BF)
    attended, logsum = att_fwd(queries, keys, keys_t, values, values_t, HD)
    stream_two = stream + mm(attended, out_full) + proj_offset
    normed_two = norm_apply(stream_two, gain_two, shift_two).astype(BF)
    expand_full = jnp.concatenate(w_exp, 1)
    hidden_pre = mm(normed_two, expand_full) + expand_offset
    activated = jax.nn.gelu(hidden_pre, approximate=False).astype(BF)
    output = swap((stream_two + mm(activated, reduce_full) + reduce_offset).astype(BF))

    grad_out = cotangent.astype(FL)
    reduce_bias_grad = jnp.sum(grad_out, 0)
    grad_act = mmt(cotangent, reduce_full)
    _, gelu_back = jax.vjp(partial(jax.nn.gelu, approximate=False), hidden_pre)
    grad_pre = gelu_back(grad_act)[0].astype(BF)
    expand_bias_grad = jnp.sum(grad_pre.astype(FL), 0)
    grad_normed_two = mmt(grad_pre, expand_full)
    _, second_back = jax.vjp(norm_apply, stream_two, gain_two, shift_two)
    grad_rows_two, second_gain_grad, second_shift_grad = second_back(grad_normed_two)
    grad_stream_two = grad_out + grad_rows_two
    grad_branch = grad_stream_two.astype(BF)
    project_bias_grad = jnp.sum(grad_branch.astype(FL), 0)
    grad_attended = mmt(grad_branch, out_full).astype(BF)
    lag = 2 if depth <= 4 else 1
    per = lambda w: w.shape[0]
    reduce_weight_grad, expand_weight_grad, project_out_grad = reduce_grads(
        (activated, normed_two, attended),
        (cotangent, grad_pre, grad_branch),
        segments(0, 0, 0, dps, per(reduce_weight), hidden, width)
        + segments(1, 1, 1, dps, per(expand_weight), width, hidden)
        + segments(2, 2, 2, dps, per(project_out), width, width),
        [reduce_weight.shape, expand_weight.shape, project_out.shape],
        depth, lag, 1,
    )
    d_q, dk_own, dk_t, dv_own, dv_t = att_bwd(
        queries, keys, keys_t, values, values_t, attended, logsum, grad_attended, HD
    )
    d_k = (dk_own + other_core(dk_t).astype(FL)).astype(BF)
    d_v = (dv_own + other_core(dv_t).astype(FL)).astype(BF)
    grad_normed_one = mmt(d_q, w_q) + mmt(d_k, w_k) + mmt(d_v, w_v)
    _, first_back = jax.vjp(norm_apply, stream, gain_one, shift_one)
    grad_rows_one, first_gain_grad, first_shift_grad = first_back(grad_normed_one)
    grad_stream = (grad_stream_two + grad_rows_one).astype(BF)
    merge_bias_grad = jnp.sum(grad_stream.astype(FL), 0)
    back = swap(grad_stream)
    seg_in = []
    for i in range(3):
        seg_in += segments(0, i, 0, dps, per(project_in), width, width, i * width)
    project_in_grad, merge_weight_grad = reduce_grads(
        (normed_one, joined),
        (d_q, d_k, d_v, grad_stream),
        seg_in + segments(1, 3, 1, dps, per(merge_weight), 2 * width, width),
        [project_in.shape, merge_weight.shape],
        depth, lag, 2,
    )
    tokens_grad = mmt(back, merge_full[:width])
    skipped_grad = mmt(back, merge_full[width:])

    big = [merge_weight_grad, project_in_grad, project_out_grad, expand_weight_grad, reduce_weight_grad]
    if seqs > 2:
        groups = [list(range(h, seqs, 2)) for h in range(2)]
        big = lax.psum(big, "seq", axis_index_groups=groups)
    vectors = [merge_bias_grad, first_gain_grad, first_shift_grad, project_bias_grad, second_gain_grad, second_shift_grad, reduce_bias_grad]
    packed = jnp.concatenate([v.reshape(dps, -1) for v in vectors + [expand_bias_grad]], 1)
    summed = lax.psum(packed, ("dp", "seq"))
    mine = lax.dynamic_index_in_dim(summed, dp, 0, keepdims=False)
    sm_out = [mine[i * piece : (i + 1) * piece] for i in range(7)]
    return (
        output, tokens_grad, skipped_grad, *big,
        sm_out[0], sm_out[1], sm_out[2], sm_out[3], sm_out[4], sm_out[5], mine[7 * piece :], sm_out[6],
    )


def solution(mesh):
    rows = P(("dp", "seq"), None)
    two = P("dp", None)
    one = P("dp")
    return jax.shard_map(
        partial(on_device, mesh.shape["dp"], mesh.shape["seq"]),
        mesh=mesh,
        in_specs=(rows, rows, rows, two, one, one, one, two, two, one, one, one, two, one, two, one),
        out_specs=(rows, rows, rows, two, two, two, two, two, one, one, one, one, one, one, one, one),
        check_vma=False,
    )
```

time: 1340 us -> 635 us (0.47)
  waiting for transfers between devices: 667 us -> 0.02 us
  Pallas kernels: 0 us -> 390 us
  blocking collectives: 202 us -> 39 us
  matrix products: 244 us -> 89.3 us
  other arithmetic: 75.9 us -> 25.5 us
  local copies, waits for them, and re-layouts: 109 us -> 69.5 us
  between operations: 16.7 us -> 1.67 us
    reduce_scatter x5 -> x0, waiting for transfers between devices: 548 us -> none  [the longest x1 181 us: on_device(): lax.psum_scatter(expand_weight_grad, 'dp', scatter_dimension=0, tiled=True)]
    pallas_call x0 -> x5, Pallas kernels: none -> 390 us  [the longest x2 177 us: reduce_grads(): pl.pallas_call(functools.partial(reduce_kernel, Z, T, L, segs, len(xs), l...]
    dot_general x21 -> x15, matrix products: 244 us -> 89.3 us  [the longest x8 55.8 us: mmt(): lax.dot_general(left, right, (((1,), (1,)), ((), ())), preferred_element_...]
    unnamed x2 -> x0, blocking collectives: 124 us -> none
    all_to_all x3 -> x0, waiting for transfers between devices: 68.5 us -> none  [the longest x1 58.7 us: on_device(): lax.all_to_all(triple, 'seq', split_axis=2, concat_axis=0, tiled=True)]
    all_to_all x1 -> x0, blocking collectives: 53.6 us -> none  [on_device(): lax.all_to_all(grad_blocks.reshape(group, 3, local_width), 'seq', split_a...]
    all_gather x5 -> x0, waiting for transfers between devices: 33.6 us -> none  [the longest x1 33.6 us: on_device(): lax.all_gather(project_in, 'dp', axis=0, tiled=True)]
    psum x1, blocking collectives: 5.84 us -> 39 us  [on_device(): summed = lax.psum(packed, ('dp', 'seq'))]
  transfers between devices with their start and end apart: 14 -> 9, of which waited for: 8 -> 0; matrix products, arithmetic and copies ran while one was open for 28% -> 15% of each run, Pallas kernels for 0% -> 53%
where the time goes in v1:
time: 635 us; the launch traced here: 625 us
  Pallas kernels  390 us (61%)
  matrix products  89.3 us (14%)
  local copies, waits for them, and re-layouts  69.5 us (11%)
  blocking collectives  39 us (6%)
  other arithmetic  25.5 us (4%)
  starting transfers between devices  9.41 us (1%)
    pallas_call x2, Pallas kernels, reduce_grads(): pl.pallas_call(functools.partial(reduce_kernel, Z, T, L, segs, len(xs), l...  177 us
    pallas_call x1, Pallas kernels, gather(): pl.pallas_call(functools.partial(gather_kernel, Z, R, rc, L), out_shape=j...  152 us
    dot_general x8, matrix products, mmt(): lax.dot_general(left, right, (((1,), (1,)), ((), ())), preferred_element_...  55.8 us
    psum x1, blocking collectives, on_device(): summed = lax.psum(packed, ('dp', 'seq'))  39 us
    pallas_call x1, Pallas kernels, att_bwd(): pl.pallas_call(functools.partial(bwd_kernel, HD), grid=(D // 128,), in_sp...  37.2 us
    dot_general x7, matrix products, mm(): return jnp.dot(left, right, preferred_element_type=FL)  33.5 us
    slice x3, local copies, waits for them, and re-layouts, whole(): return gathered[:, bounds[i]:bounds[i + 1]].reshape(-1, width)  24 us
    pallas_call x1, Pallas kernels, att_fwd(): pl.pallas_call(functools.partial(fwd_kernel, HD), grid=(D // 128,), in_sp...  23.6 us
  transfers between devices with their start and end apart: 9, of which 0 were waited for; matrix products, arithmetic and copies ran while one was open for 15% of the time, Pallas kernels for 53%

profile of v1, /device:TPU:0, one launch (start us, length us, event | category | flops | bytes accessed | tf_op | source)
XLA Modules:
  0.0 624.7 jit_solution(16902417333800979976)
XLA Ops:
  0.7 1.8 collective-permute-start
  3.2 1.7 collective-permute-start.5
  4.9 5.4 concatenate.16
  10.3 1.0 constant_dynamic-update-slice_fusion.2
  17.0 1.2 copy-done.17
  18.2 152.3 %shard_map.279 = bf16[4,2,2,928,1024]{4,3,2,1,0:T(8,128)(2,1)} custom-call(bf16[928,1024]{1,0:T(8,128)(2,1)} %copy-done.17), custom_call_target="tpu_custom_call" | custom-call | tf_op jit(solution)/shard_map/pallas_call | solution.py:112
  170.5 4.7 slice.186
  176.6 11.3 %fusion.21 = (bf16[16,64,1024]{2,1,0:T(8,128)(2,1)}, bf16[16,64,1024]{2,1,0:T(8,128)(2,1)}, bf16[16,64,1024]{2,1,0:T(8,128)(2,1)}, bf16[16,64,1024]{2,1,0:T(8,12...) fusion(bf16[16,928,1024]{2,1,0:T(8,128)(2,1)} %bitcast.61), kind=kLoop, calls=%fused_computation.93 | loop fusion | bytes 33554432 | tf_op jit(solution)/shard_map/slice | solution.py:471
  188.1 1.9 copy-done.30
  190.1 2.6 copy-done.16
  192.7 2.6 add_reduce_fusion
  196.4 2.4 convolution_convert_fusion.1.vo
  198.8 2.4 convolution_convert_fusion.2.ko
  201.2 1.2 collective-permute-start.2
  202.3 8.0 %slice.203 = bf16[16,256,1024]{2,1,0:T(8,128)(2,1)} slice(bf16[16,928,1024]{2,1,0:T(8,128)(2,1)} %bitcast.62), slice={[0:16], [672:928], [0:1024]} | slice | bytes 16777216 | tf_op jit(solution)/shard_map/slice | solution.py:471
  211.3 2.5 convert_reduce_fusion.1
  213.8 4.1 convolution_convert_fusion.3.qr
  217.8 23.6 %shard_map.280 = (bf16[552,1024]{1,0:T(8,128)(2,1)}, f32[552,1024]{1,0:T(8,128)}) custom-call(bf16[552,1024]{1,0:T(8,128)(2,1)} %convolution_convert_fusion.3.qr, bf16[552,1024]{1,0:T(8,128)(2,1)} %convolution_convert_fusion.2.ko, bf16[552,1024]{1,0:T(8,128)(2,1)} %collective-permute-done.2.kt, bf16[552,1024]{1,0:T(8,128)(2,1)} %convolution_convert_fusion.1.vo, ...), custom_call_target="tpu_custom_call" | custom-call | tf_op jit(solution)/shard_map/pallas_call | solution.py:361
  241.5 2.7 fusion.23
  245.1 1.9 copy-done.26
  247.0 8.0 %fusion.7 = f32[552,4096]{1,0:T(8,128)S(1)} fusion(bf16[552,1024]{1,0:T(8,128)(2,1)S(1)} %add_convert_fusion.5.refs_1_, bf16[1024,1024]{1,0:T(8,128)(2,1)} %bitcast.77, bf16[1024,1024]{1,0:T(8,128)(2,1)} %bitcast.79, bf16[1024,1024]{1,0:T(8,128)(2,1)} %bitcast.81, bf16[1024,1024]{1,0:T(8,128)(2,1)S(1)} %bitcast.75), kind=kOutput, calls=%fused_computation.47 | convolution fusion | flops 4664066048 | bytes 18563072 | tf_op jit(solution)/shard_map/dot_general | solution.py:408
  255.0 30.0 %convert_reduce_fusion = (f32[4096]{0:T(1024)}, bf16[552,4096]{1,0:T(8,128)(2,1)}, f32[552,4096]{1,0:T(8,128)}) fusion(f32[552,4096]{1,0:T(8,128)S(1)} %fusion.7, f32[4096]{0:T(1024)S(1)} %bitcast.87, bf16[552,1024]{1,0:T(8,128)(2,1)S(1)} %get-tuple-element.50.refs_3_, bf16[4096,1024]{1,0:T(8,128)(2,1)} %bitcast.66), kind=kOutput, calls=%fused_computation.2 | convolution fusion | flops 4800081920 | bytes 32161792 | tf_op jit(solution)/shard_map/dot_general | solution.py:412
  285.0 10.0 %multiply_reduce_fusion = (f32[1024]{0:T(1024)}, f32[552]{0:T(1024)S(1)}, f32[1024]{0:T(1024)}, f32[552,1024]{1,0:T(8,128)S(1)}) fusion(f32[552,1024]{1,0:T(8,128)S(1)} %get-tuple-element.87, f32[552]{0:T(1024)S(1)} %fusion.12, f32[552]{0:T(1024)S(1)} %broadcast_multiply_fusion, f32[1024]{0:T(1024)S(1)} %mul.161, ...), kind=kOutput, calls=%fused_computation.24 | convolution fusion | flops 4668585472 | bytes 17451488 | tf_op jit(solution)/shard_map/dot_general | solution.py:412
  295.8 10.4 %multiply_convert_fusion.refs_0_ = bf16[552,4096]{1,0:T(8,128)(2,1)} fusion(f32[552,4096]{1,0:T(8,128)} %get-tuple-element.48, f32[552,4096]{1,0:T(8,128)} %copy-done.5, f32[4096]{0:T(1024)S(1)} %bitcast.88), kind=kLoop, calls=%fused_computation.4 | loop fusion | flops 9043968 | bytes 22626304 | tf_op jit(solution)/shard_map/convert_element_type | solution.py:495
  306.2 1.0 convert_reduce_fusion.2
  307.8 2.4 convolution_convert_fusion.g_ref
  310.2 37.2 %shard_map.281 = (bf16[552,1024]{1,0:T(8,128)(2,1)}, f32[552,1024]{1,0:T(8,128)}, bf16[552,1024]{1,0:T(8,128)(2,1)}, f32[552,1024]{1,0:T(8,128)}, bf16[552,1024]{1,0:T(8,128)(2,1)}) custom-call(bf16[552,1024]{1,0:T(8,128)(2,1)} %convolution_convert_fusion.3.qr, bf16[552,1024]{1,0:T(8,128)(2,1)} %convolution_convert_fusion.2.ko, ...), custom_call_target="tpu_custom_call" | custom-call | tf_op jit(solution)/shard_map/pallas_call | solution.py:396
  348.0 11.3 %add_convert_fusion.4 = bf16[552,1024]{1,0:T(8,128)(2,1)} fusion(f32[552,1024]{1,0:T(8,128)} %copy-done.2, bf16[552,4096]{1,0:T(8,128)(2,1)} %multiply_convert_fusion.refs_0_, bf16[4096,1024]{1,0:T(8,128)(2,1)} %bitcast.67, f32[1024]{0:T(1024)S(1)} %copy-done.50), kind=kOutput, calls=%fused_computation.34 | convolution fusion | flops 4632207360 | bytes 16306176 | tf_op jit(solution)/shard_map/dot_general | solution.py:408
  359.3 1.7 collective-permute-start.4
  361.0 1.4 fusion.24
  363.1 1.1 copy-done.21
  364.3 1.4 fusion.25
  366.7 1.2 copy-done.1
  368.6 2.5 multiply_reduce_fusion.1
  372.0 2.1 convert_reduce_fusion.3
  374.1 1.7 collective-permute-start.8
  375.8 5.0 fusion.20
  381.5 1.6 pad_maximum_fusion.1.refs_1_
  383.0 107.5 %shard_map.283 = (f32[256,1024]{1,0:T(8,128)}, f32[64,4096]{1,0:T(8,128)}, f32[64,1024]{1,0:T(8,128)}) custom-call(bf16[552,4096]{1,0:T(8,128)(2,1)} %multiply_convert_fusion.refs_0_, bf16[552,1024]{1,0:T(8,128)(2,1)} %copy-done.9, bf16[552,1024]{1,0:T(8,128)(2,1)} %get-tuple-element.28.o_ref.refs_2_, bf16[552,1024]{1,0:T(8,128)(2,1)} %copy-done.3, ...), custom_call_target="tpu_custom_call" | custom-call | tf_op jit(solution)/shard_map/pallas_call | solution.py:325
  490.6 1.3 reshape.195
  491.9 1.3 reshape.192
  493.2 1.3 reshape.193
  494.6 1.3 reshape.191
  495.9 69.8 %shard_map.282 = (f32[64,3072]{1,0:T(8,128)}, f32[128,1024]{1,0:T(8,128)}) custom-call(bf16[552,1024]{1,0:T(8,128)(2,1)} %copy-done.15, bf16[552,2048]{1,0:T(8,128)(2,1)} %pad_maximum_fusion.1.refs_1_, bf16[552,1024]{1,0:T(8,128)(2,1)} %get-tuple-element.30.refs_2_, bf16[552,1024]{1,0:T(8,128)(2,1)} %copy-done.14, bf16[552,1024]{1,0:T(8,128)(2,1)} %copy-done.4, ...), custom_call_target="tpu_custom_call" | custom-call | tf_op jit(solution)/shard_map/pallas_call | solution.py:325
  569.0 39.0 %psum.7 = f32[16,704]{1,0:T(8,128)S(1)} all-reduce(f32[16,704]{1,0:T(8,128)S(1)} %concatenate.19), channel_id=1, replica_groups=mesh['dp'=16,'seq'=2] {'dp','seq'}, use_global_device_ids=true, to_apply=%region_16.17 | all-reduce | flops 11264 | bytes 90112 | tf_op jit(solution)/shard_map/psum | solution.py:552
  609.2 2.4 broadcast_select_fusion.2
  611.6 4.2 fusion.9
  615.8 4.1 fusion.10
  (162 shorter events, 25.6 us)
Async XLA Ops:
  0.6 16.2 %copy-start.35 = (bf16[64,4096]{1,0:T(8,128)(2,1)S(1)}, bf16[64,4096]{1,0:T(8,128)(2,1)}, u32[]{:S(2)}) copy-start(bf16[64,4096]{1,0:T(8,128)(2,1)} %param.28) | copy-start | bytes 1572868
  0.7 187.2 %collective-permute-start = (bf16[552,1024]{1,0:T(8,128)(2,1)}, bf16[552,1024]{1,0:T(8,128)(2,1)}, u32[]{:S(2)}, u32[]{:S(2)}) collective-permute-start(bf16[552,1024]{1,0:T(8,128)(2,1)} %param.16), channel_id=1, source_target_pairs={{1,2},{2,1},{5,6},{6,5},{9,10},{10,9},{13,14},{14,13},{17,18},{18,... | collective-permute-start | bytes 3391496 | tf_op jit(solution)/shard_map/ppermute | solution.py:450
  2.5 185.6 %collective-permute-start.1 = (bf16[552,1024]{1,0:T(8,128)(2,1)}, bf16[552,1024]{1,0:T(8,128)(2,1)S(1)}, u32[]{:S(2)}, u32[]{:S(2)}) collective-permute-start(bf16[552,1024]{1,0:T(8,128)(2,1)} %param.17), channel_id=1, source_target_pairs={{1,2},{2,1},{5,6},{6,5},{9,10},{10,9},{13,14},{14,13},{17,18},{18,... | collective-permute-start | bytes 3391496 | tf_op jit(solution)/shard_map/ppermute | solution.py:450
  3.2 208.1 %collective-permute-start.5 = (bf16[552,1024]{1,0:T(8,128)(2,1)}, bf16[552,1024]{1,0:T(8,128)(2,1)}, u32[]{:S(2)}, u32[]{:S(2)}) collective-permute-start(bf16[552,1024]{1,0:T(8,128)(2,1)} %param.18), channel_id=1, source_target_pairs={{1,2},{2,1},{5,6},{6,5},{9,10},{10,9},{13,14},{14,13},{17,18},{18,... | collective-permute-start | bytes 3391496 | tf_op jit(solution)/shard_map/ppermute | solution.py:450
  10.3 6.6 %copy-start.36 = (bf16[256,1024]{1,0:T(8,128)(2,1)S(1)}, bf16[256,1024]{1,0:T(8,128)(2,1)}, u32[]{:S(2)}) copy-start(bf16[256,1024]{1,0:T(8,128)(2,1)} %param.30) | copy-start | bytes 1572868
  176.4 65.0 %copy-start.39 = (f32[1024]{0:T(1024)}, f32[1024]{0:T(1024)S(1)}, u32[]{:S(2)}) copy-start(f32[1024]{0:T(1024)S(1)} %add.123) | copy-start | bytes 12292
  176.5 19.3 %copy-start.43 = (f32[1024]{0:T(1024)}, f32[1024]{0:T(1024)S(1)}, u32[]{:S(2)}) copy-start(f32[1024]{0:T(1024)S(1)} %mul.155) | copy-start | bytes 12292
  176.6 11.3 %copy-start.29 = (bf16[552,1024]{1,0:T(8,128)(2,1)S(1)}, bf16[552,1024]{1,0:T(8,128)(2,1)}, u32[]{:S(2)}) copy-start(bf16[552,1024]{1,0:T(8,128)(2,1)} %param.16) | copy-start | bytes 3391492
  187.8 8.6 %copy-start.6 = (bf16[16,64,1024]{2,1,0:T(8,128)(2,1)}, bf16[16,64,1024]{2,1,0:T(8,128)(2,1)S(1)}, u32[]{:S(2)}) copy-start(bf16[16,64,1024]{2,1,0:T(8,128)(2,1)S(1)} %get-tuple-element.67) | copy-start | bytes 6291460
  187.8 10.9 %copy-start.20 = (bf16[16,64,1024]{2,1,0:T(8,128)(2,1)}, bf16[16,64,1024]{2,1,0:T(8,128)(2,1)S(1)}, u32[]{:S(2)}) copy-start(bf16[16,64,1024]{2,1,0:T(8,128)(2,1)S(1)} %get-tuple-element.68) | copy-start | bytes 6291460
  187.9 4.8 copy-start.16
  188.1 7.2 %copy-start.10 = (bf16[552,1024]{1,0:T(8,128)(2,1)}, bf16[552,1024]{1,0:T(8,128)(2,1)S(1)}, u32[]{:S(2)}) copy-start(bf16[552,1024]{1,0:T(8,128)(2,1)S(1)} %broadcast_select_fusion.4) | copy-start | bytes 3391492
  190.1 5.2 copy-start.12
  195.3 46.1 %copy-start = (f32[552,1024]{1,0:T(8,128)}, f32[552,1024]{1,0:T(8,128)S(1)}, u32[]{:S(2)}) copy-start(f32[552,1024]{1,0:T(8,128)S(1)} %get-tuple-element.85) | copy-start | bytes 6782980
  195.8 3.0 copy-start.47
  195.8 3.0 copy-start.45
  196.4 2.4 copy-start.15
  201.2 16.7 %collective-permute-start.2 = (bf16[552,1024]{1,0:T(8,128)(2,1)}, bf16[552,1024]{1,0:T(8,128)(2,1)}, u32[]{:S(2)}, u32[]{:S(2)}) collective-permute-start(bf16[552,1024]{1,0:T(8,128)(2,1)} %convolution_convert_fusion.2.ko), channel_id=1, source_target_pairs={{0,2},{1,3},{2,0},{3,1},{4,6},{5,7},{6,4},{7,5},{8,10},{9,11},{10,... | collective-permute-start | bytes 3391496 | tf_op jit(solution)/shard_map/ppermute | solution.py:453
  202.3 15.5 %collective-permute-start.3 = (bf16[552,1024]{1,0:T(8,128)(2,1)}, bf16[552,1024]{1,0:T(8,128)(2,1)}, u32[]{:S(2)}, u32[]{:S(2)}) collective-permute-start(bf16[552,1024]{1,0:T(8,128)(2,1)} %convolution_convert_fusion.1.vo), channel_id=1, source_target_pairs={{0,2},{1,3},{2,0},{3,1},{4,6},{5,7},{6,4},{7,5},{8,10},{9,11},{10,... | collective-permute-start | bytes 3391496 | tf_op jit(solution)/shard_map/ppermute | solution.py:453
  211.3 2.5 copy-start.22
  213.7 158.2 %copy-start.3 = (bf16[552,1024]{1,0:T(8,128)(2,1)}, bf16[552,1024]{1,0:T(8,128)(2,1)S(1)}, u32[]{:S(2)}) copy-start(bf16[552,1024]{1,0:T(8,128)(2,1)S(1)} %get-tuple-element.50.refs_3_) | copy-start | bytes 3391492
  217.8 23.7 %copy-start.24 = (bf16[16,64,1024]{2,1,0:T(8,128)(2,1)S(1)}, bf16[16,64,1024]{2,1,0:T(8,128)(2,1)}, u32[]{:S(2)}) copy-start(bf16[16,64,1024]{2,1,0:T(8,128)(2,1)} %get-tuple-element.66) | copy-start | bytes 6291460
  244.2 50.8 %copy-start.2 = (f32[552,1024]{1,0:T(8,128)}, f32[552,1024]{1,0:T(8,128)S(1)}, u32[]{:S(2)}) copy-start(f32[552,1024]{1,0:T(8,128)S(1)} %get-tuple-element.87) | copy-start | bytes 6782980
  244.6 2.4 copy-start.26
  245.1 9.9 %copy-start.9 = (bf16[552,1024]{1,0:T(8,128)(2,1)}, bf16[552,1024]{1,0:T(8,128)(2,1)S(1)}, u32[]{:S(2)}) copy-start(bf16[552,1024]{1,0:T(8,128)(2,1)S(1)} %add_convert_fusion.5.refs_1_) | copy-start | bytes 3391492
  255.0 30.0 %copy-start.5 = (f32[552,4096]{1,0:T(8,128)}, f32[552,4096]{1,0:T(8,128)S(1)}, u32[]{:S(2)}) copy-start(f32[552,4096]{1,0:T(8,128)S(1)} %fusion.7) | copy-start | bytes 27131908
  307.2 3.0 copy-start.8
  310.2 37.9 %copy-start.50 = (f32[1024]{0:T(1024)S(1)}, f32[1024]{0:T(1024)}, u32[]{:S(2)}) copy-start(f32[1024]{0:T(1024)} %add.142) | copy-start | bytes 12292
  347.4 15.0 %collective-permute-start.6 = (bf16[552,1024]{1,0:T(8,128)(2,1)}, bf16[552,1024]{1,0:T(8,128)(2,1)S(1)}, u32[]{:S(2)}, u32[]{:S(2)}) collective-permute-start(bf16[552,1024]{1,0:T(8,128)(2,1)} %get-tuple-element.32), channel_id=1, source_target_pairs={{0,2},{1,3},{2,0},{3,1},{4,6},{5,7},{6,4},{7,5},{8,10},{9,11},{10,... | collective-permute-start | bytes 3391496 | tf_op jit(solution)/shard_map/ppermute | solution.py:453
  347.9 13.1 %copy-start.23 = (bf16[16,64,1024]{2,1,0:T(8,128)(2,1)S(1)}, bf16[16,64,1024]{2,1,0:T(8,128)(2,1)}, u32[]{:S(2)}) copy-start(bf16[16,64,1024]{2,1,0:T(8,128)(2,1)} %get-tuple-element.69) | copy-start | bytes 6291460
  347.9 13.1 %copy-start.31 = (bf16[552,1024]{1,0:T(8,128)(2,1)S(1)}, bf16[552,1024]{1,0:T(8,128)(2,1)}, u32[]{:S(2)}) copy-start(bf16[552,1024]{1,0:T(8,128)(2,1)} %get-tuple-element.30.refs_2_) | copy-start | bytes 3391492
  347.9 17.7 %collective-permute-start.7 = (bf16[552,1024]{1,0:T(8,128)(2,1)}, bf16[552,1024]{1,0:T(8,128)(2,1)S(1)}, u32[]{:S(2)}, u32[]{:S(2)}) collective-permute-start(bf16[552,1024]{1,0:T(8,128)(2,1)} %get-tuple-element.34), channel_id=1, source_target_pairs={{0,2},{1,3},{2,0},{3,1},{4,6},{5,7},{6,4},{7,5},{8,10},{9,11},{10,... | collective-permute-start | bytes 3391496 | tf_op jit(solution)/shard_map/ppermute | solution.py:453
  359.3 249.9 %collective-permute-start.4 = (bf16[552,1024]{1,0:T(8,128)(2,1)}, bf16[552,1024]{1,0:T(8,128)(2,1)}, u32[]{:S(2)}, u32[]{:S(2)}) collective-permute-start(bf16[552,1024]{1,0:T(8,128)(2,1)} %add_convert_fusion.4), channel_id=1, source_target_pairs={{1,2},{2,1},{5,6},{6,5},{9,10},{10,9},{13,14},{14,13},{17,18},{18,... | collective-permute-start | bytes 3391496 | tf_op jit(solution)/shard_map/ppermute | solution.py:450
  366.3 2.3 copy-start.7
  366.3 2.3 copy-start.40
  366.3 2.3 copy-start.42
  368.6 2.5 copy-start.4
  368.6 2.5 copy-start.48
  374.1 237.5 %collective-permute-start.8 = (bf16[552,1024]{1,0:T(8,128)(2,1)}, bf16[552,1024]{1,0:T(8,128)(2,1)}, u32[]{:S(2)}, u32[]{:S(2)}) collective-permute-start(bf16[552,1024]{1,0:T(8,128)(2,1)} %get-tuple-element.54.refs_5_), channel_id=1, source_target_pairs={{1,2},{2,1},{5,6},{6,5},{9,10},{10,9},{13,14},{14,13},{17,18},{18,... | collective-permute-start | bytes 3391496 | tf_op jit(solution)/shard_map/ppermute | solution.py:450
  375.8 5.0 copy-start.49
  375.8 5.7 copy-start.11
  375.8 5.7 copy-start.13
  565.7 45.9 %copy-start.28 = (bf16[8,128,1024]{2,1,0:T(8,128)(2,1)S(1)}, bf16[8,128,1024]{2,1,0:T(8,128)(2,1)}, u32[]{:S(2)}) copy-start(bf16[8,128,1024]{2,1,0:T(8,128)(2,1)} %get-tuple-element.60) | copy-start | bytes 6291460
  611.6 4.2 copy-start.27
  615.8 4.1 copy-start.37
  615.8 4.9 copy-start.34
  619.9 2.4 copy-start.33
  620.7 2.6 copy-start.32
  (12 other events, 20.5 us)
